TPU v7x, 32 devices: a whole 2x2x4 slice. The times are simulated.
32 devices in a mesh: dop: 2 (over core), tm: 16 (over z, y, x).
Axes of the slice: x: 2, y: 2, z: 4, core: 2. Of those that a mesh axis runs over, the one named last changes fastest.
Arguments:
- surveillance: bfloat16 [2, 16, 8192], P(None, 'tm', 'dop'), may hold values from -6 to 6
- reference_signal: bfloat16 [2, 16, 8192], P(None, 'tm', 'dop'), may hold values from -6 to 6
Outputs:
- ambiguity: float32 [2048, 2, 512], P('tm', None, 'dop')
All inputs are finite; a program needn't handle non-finite values.
Results may differ from a plain program's by a relative error of at most 0.0029.
Values may be sent and summed in bfloat16 or wider, within the bound.
A program may use at most 128 MiB of HBM per device.

v0:
```python
import math

import jax
import jax.numpy as jnp
from jax import lax
from jax.sharding import PartitionSpec as P

F = 512
LAGS = 2048
BLOCK = 8192


def from_behind(value, axis, steps):
    count = lax.axis_size(axis)
    first, last = (max(0, -steps), min(count, count - steps))
    return lax.ppermute(value, axis, [(source, source + steps) for source in range(first, last)])


def toeplitz_rows(segment, height, breadth):
    length = height + breadth - 1
    repeated = jnp.tile(segment, (1, height + 1))[:, : height * (length + 1)]
    return repeated.reshape(2, height, length + 1)[:, :, :breadth]


def mix_rows(samples, sample_index, doppler, window):
    phase_step = jnp.mod(doppler[:, None] * sample_index[None, :], window)
    phase_angle = phase_step.astype(jnp.float32) * (2.0 * math.pi / window)
    cosine = jnp.cos(phase_angle)
    sine_part = jnp.sin(phase_angle)
    real_in = samples[0].astype(jnp.float32)[None, :]
    imag_in = samples[1].astype(jnp.float32)[None, :]
    mixed_real = (real_in * cosine + imag_in * sine_part).astype(jnp.bfloat16)
    mixed_imag = (imag_in * cosine - real_in * sine_part).astype(jnp.bfloat16)
    upper_half = jnp.concatenate([mixed_real, mixed_imag], 1)
    lower_half = jnp.concatenate([mixed_imag, -mixed_real], 1)
    return jnp.concatenate([upper_half, lower_half], 0)


def lag_product(toeplitz, mixed):
    height = toeplitz.shape[1]
    stacked = toeplitz.reshape(2 * height, toeplitz.shape[2])
    return lax.dot_general(
        stacked, mixed, (((0,), (1,)), ((), ())), preferred_element_type=jnp.float32
    )


def on_device(surveillance, reference_signal):
    pieces = surveillance.shape[2]
    blocks_here = surveillance.shape[1]
    time_devices = lax.axis_size("tm")
    window = BLOCK * blocks_here * time_devices
    lag_rows = LAGS // time_devices
    full_block = lax.all_gather(reference_signal, "dop", axis=2, tiled=True)
    bin_count = F
    row_shift = lax.axis_index("dop") * pieces
    block_tail = full_block[:, -1, BLOCK - LAGS + 1 :]
    earlier = from_behind(block_tail, "tm", 1)
    earlier_tails = jnp.concatenate(
        [earlier[:, None, :], full_block[:, :-1, BLOCK - LAGS + 1 :]], 1
    )
    extended = jnp.concatenate([earlier_tails, full_block], 2)
    row_count = surveillance.shape[2]
    height = min(512, row_count)
    sub_count = row_count // height
    doppler = jnp.arange(bin_count, dtype=jnp.int32) - F // 2
    block_start = lax.axis_index("tm") * blocks_here

    def one_turn(turn_no, running):
        block_no = turn_no // sub_count
        inside = turn_no % sub_count * height
        offset = row_shift + inside
        ext_row = lax.dynamic_index_in_dim(extended, block_no, 1, keepdims=False)
        segment = lax.dynamic_slice_in_dim(
            ext_row, offset, height + lag_rows * lax.axis_size("tm") - 1, 1
        )[:, ::-1]
        toeplitz = toeplitz_rows(segment, height, lag_rows * lax.axis_size("tm"))
        signal_row = lax.dynamic_index_in_dim(surveillance, block_no, 1, keepdims=False)
        samples = lax.dynamic_slice_in_dim(signal_row, inside, height, 1)[:, ::-1]
        sample_index = (
            (block_start + block_no) * BLOCK
            + offset
            + height
            - 1
            - jnp.arange(height, dtype=jnp.int32)
        )
        return running + lag_product(toeplitz, mix_rows(samples, sample_index, doppler, window))

    partial_value = lax.psum_scatter(
        lax.fori_loop(
            0,
            blocks_here * sub_count,
            one_turn,
            jnp.zeros((lag_rows * lax.axis_size("tm"), 2 * bin_count), jnp.float32),
        ),
        "tm",
        scatter_dimension=0,
        tiled=True,
    )
    result = lax.psum_scatter(
        partial_value.reshape(lag_rows, 2, F), "dop", scatter_dimension=2, tiled=True
    )
    return result * (1.0 / math.sqrt(window))


def solution(mesh):
    return jax.shard_map(
        on_device,
        mesh=mesh,
        in_specs=(P(None, "tm", "dop"), P(None, "tm", "dop")),
        out_specs=P("tm", None, "dop"),
        check_vma=False,
    )
```

profile of v0, /device:TPU:0, one launch (start us, length us, event | category | flops | bytes accessed | tf_op | source)
XLA Modules:
  0.0 706.5 jit_solution(10309439441344766599)
XLA Ops:
  8.8 4.7 collective-permute-start
  15.0 410.3 %while.19 = (s32[]{:T(128)}, f32[2048,1024]{1,0:T(8,128)}, s32[]{:T(128)}, bf16[2,1,10239]{2,0,1:T(2,128)(2,1)S(1)}, bf16[2,1,4096]{2,0,1:T(2,128)(2,1)}, /*inde...) while((s32[]{:T(128)}, f32[2048,1024]{1,0:T(8,128)}, ...), condition=%wide.region_1.2_spmd.clone, body=%wide.region_0.1_spmd.clone.sunk | while | flops 4318824448 | bytes 143802912 | solution.py:89
  18.6 4.7 fusion.22
  23.3 4.8 add_convert_fusion.2
  28.0 2.8 tile.32
  30.8 12.7 %reshape.83 = bf16[2625534]{0:T(1024)(128)(2,1)} reshape(bf16[2,513,2559]{2,1,0:T(8,128)(2,1)} %tile.32) | data formatting | bytes 10502136 | tf_op jit(solution)/shard_map/while
  43.5 7.7 %tile.33 = bf16[2,1312767]{1,0:T(2,128)(2,1)} reshape(bf16[2625534]{0:T(1024)(128)(2,1)} %reshape.83) | data formatting | bytes 10502136 | tf_op jit(solution)/shard_map/while/body/eval_jaxpr/tile | solution.py:21
  56.3 6.8 select_add_fusion.2
  63.1 3.2 copy-done
  69.9 4.7 fusion.22
  74.6 4.8 add_convert_fusion.2
  79.3 2.8 tile.32
  82.1 12.7 %reshape.83 = bf16[2625534]{0:T(1024)(128)(2,1)} reshape(bf16[2,513,2559]{2,1,0:T(8,128)(2,1)} %tile.32) | data formatting | bytes 10502136 | tf_op jit(solution)/shard_map/while
  94.8 7.7 %tile.33 = bf16[2,1312767]{1,0:T(2,128)(2,1)} reshape(bf16[2625534]{0:T(1024)(128)(2,1)} %reshape.83) | data formatting | bytes 10502136 | tf_op jit(solution)/shard_map/while/body/eval_jaxpr/tile | solution.py:21
  107.6 6.8 select_add_fusion.2
  114.4 3.2 copy-done
  121.2 4.7 fusion.22
  125.8 4.8 add_convert_fusion.2
  130.6 2.8 tile.32
  133.4 12.7 %reshape.83 = bf16[2625534]{0:T(1024)(128)(2,1)} reshape(bf16[2,513,2559]{2,1,0:T(8,128)(2,1)} %tile.32) | data formatting | bytes 10502136 | tf_op jit(solution)/shard_map/while
  146.1 7.7 %tile.33 = bf16[2,1312767]{1,0:T(2,128)(2,1)} reshape(bf16[2625534]{0:T(1024)(128)(2,1)} %reshape.83) | data formatting | bytes 10502136 | tf_op jit(solution)/shard_map/while/body/eval_jaxpr/tile | solution.py:21
  158.9 6.8 select_add_fusion.2
  165.7 3.2 copy-done
  172.5 4.7 fusion.22
  177.1 4.8 add_convert_fusion.2
  181.9 2.8 tile.32
  184.7 12.7 %reshape.83 = bf16[2625534]{0:T(1024)(128)(2,1)} reshape(bf16[2,513,2559]{2,1,0:T(8,128)(2,1)} %tile.32) | data formatting | bytes 10502136 | tf_op jit(solution)/shard_map/while
  197.4 7.7 %tile.33 = bf16[2,1312767]{1,0:T(2,128)(2,1)} reshape(bf16[2625534]{0:T(1024)(128)(2,1)} %reshape.83) | data formatting | bytes 10502136 | tf_op jit(solution)/shard_map/while/body/eval_jaxpr/tile | solution.py:21
  210.2 6.8 select_add_fusion.2
  217.0 3.2 copy-done
  223.7 4.7 fusion.22
  228.4 4.8 add_convert_fusion.2
  233.2 2.8 tile.32
  236.0 12.7 %reshape.83 = bf16[2625534]{0:T(1024)(128)(2,1)} reshape(bf16[2,513,2559]{2,1,0:T(8,128)(2,1)} %tile.32) | data formatting | bytes 10502136 | tf_op jit(solution)/shard_map/while
  248.6 7.7 %tile.33 = bf16[2,1312767]{1,0:T(2,128)(2,1)} reshape(bf16[2625534]{0:T(1024)(128)(2,1)} %reshape.83) | data formatting | bytes 10502136 | tf_op jit(solution)/shard_map/while/body/eval_jaxpr/tile | solution.py:21
  261.5 6.8 select_add_fusion.2
  268.3 3.2 copy-done
  275.0 4.7 fusion.22
  279.7 4.8 add_convert_fusion.2
  284.5 2.8 tile.32
  287.2 12.7 %reshape.83 = bf16[2625534]{0:T(1024)(128)(2,1)} reshape(bf16[2,513,2559]{2,1,0:T(8,128)(2,1)} %tile.32) | data formatting | bytes 10502136 | tf_op jit(solution)/shard_map/while
  299.9 7.7 %tile.33 = bf16[2,1312767]{1,0:T(2,128)(2,1)} reshape(bf16[2625534]{0:T(1024)(128)(2,1)} %reshape.83) | data formatting | bytes 10502136 | tf_op jit(solution)/shard_map/while/body/eval_jaxpr/tile | solution.py:21
  312.7 6.8 select_add_fusion.2
  319.5 3.2 copy-done
  326.3 4.7 fusion.22
  331.0 4.8 add_convert_fusion.2
  335.7 2.8 tile.32
  338.5 12.7 %reshape.83 = bf16[2625534]{0:T(1024)(128)(2,1)} reshape(bf16[2,513,2559]{2,1,0:T(8,128)(2,1)} %tile.32) | data formatting | bytes 10502136 | tf_op jit(solution)/shard_map/while
  351.2 7.7 %tile.33 = bf16[2,1312767]{1,0:T(2,128)(2,1)} reshape(bf16[2625534]{0:T(1024)(128)(2,1)} %reshape.83) | data formatting | bytes 10502136 | tf_op jit(solution)/shard_map/while/body/eval_jaxpr/tile | solution.py:21
  364.0 6.8 select_add_fusion.2
  370.8 3.2 copy-done
  377.6 4.7 fusion.22
  382.3 4.8 add_convert_fusion.2
  387.0 2.8 tile.32
  389.8 12.7 %reshape.83 = bf16[2625534]{0:T(1024)(128)(2,1)} reshape(bf16[2,513,2559]{2,1,0:T(8,128)(2,1)} %tile.32) | data formatting | bytes 10502136 | tf_op jit(solution)/shard_map/while
  402.5 7.7 %tile.33 = bf16[2,1312767]{1,0:T(2,128)(2,1)} reshape(bf16[2625534]{0:T(1024)(128)(2,1)} %reshape.83) | data formatting | bytes 10502136 | tf_op jit(solution)/shard_map/while/body/eval_jaxpr/tile | solution.py:21
  415.3 6.8 select_add_fusion.2
  422.1 3.2 copy-done
  425.4 180.0 %reduce-scatter.5.cloned.1.call-done = f32[128,1024]{1,0:T(8,128)} async-done(((f32[2048,1024]{1,0:T(8,128)}), f32[128,1024]{1,0:T(8,128)}) %reduce-scatter.5.cloned.1.call-update) | async-done | bytes 524304 | tf_op jit(solution)/shard_map/reduce_scatter | solution.py:88
  606.9 26.2 %copy.5 = f32[128,2,512]{1,0,2:T(8,128)} copy(f32[128,2,512]{2,1,0:T(2,128)S(1)} %reshape.71) | data formatting | bytes 1048576
  633.1 24.6 %reshape.78 = f32[512,256]{1,0:T(8,128)} reshape(f32[512,128,2]{2,1,0:T(8,128)} %bitcast.40) | data formatting | bytes 1048576
  657.7 10.5 %reduce-scatter.7.cloned.1.call-done = f32[256,256]{1,0:T(8,128)} async-done(((f32[512,256]{1,0:T(8,128)}), f32[256,256]{1,0:T(8,128)}) %reduce-scatter.7.cloned.1.call-update) | async-done | bytes 262160
  668.2 18.8 %reshape.79 = f32[256,128,2]{2,1,0:T(8,128)} reshape(f32[256,256]{1,0:T(8,128)} %reduce-scatter.7.cloned.1.call-done) | data formatting | bytes 524288
  687.0 11.8 %copy.6 = f32[128,2,256]{2,1,0:T(2,128)S(1)} copy(f32[128,2,256]{1,0,2:T(8,128)} %bitcast.42) | data formatting | bytes 524288
  (163 shorter events, 75.7 us)
Async XLA Ops:
  6.5 598.8 %reduce-scatter.5.cloned.1.call-start = ((), (), s32[]{:S(2)}) async-start(), calls=%async_computation.2 | async-start | bytes 8912896 | tf_op jit(solution)/shard_map/reduce_scatter | solution.py:88
  8.8 6.1 collective-permute-start
  51.2 2.5 slice-start
  51.2 3.9 slice-start.1
  53.6 2.7 slice-start.2
  63.1 3.2 copy-start
  102.4 2.5 slice-start
  102.4 3.9 slice-start.1
  104.9 2.7 slice-start.2
  114.4 3.2 copy-start
  153.7 2.5 slice-start
  153.7 3.9 slice-start.1
  156.2 2.7 slice-start.2
  165.7 3.2 copy-start
  205.0 2.5 slice-start
  205.0 3.9 slice-start.1
  207.5 2.7 slice-start.2
  217.0 3.2 copy-start
  256.3 2.5 slice-start
  256.3 3.9 slice-start.1
  258.8 2.7 slice-start.2
  268.2 3.2 copy-start
  307.6 2.5 slice-start
  307.6 3.9 slice-start.1
  310.1 2.7 slice-start.2
  319.5 3.2 copy-start
  358.9 2.5 slice-start
  358.9 3.9 slice-start.1
  361.3 2.7 slice-start.2
  370.8 3.2 copy-start
  410.1 2.5 slice-start
  410.1 3.9 slice-start.1
  412.6 2.7 slice-start.2
  422.1 3.2 copy-start
  425.3 242.9 %reduce-scatter.7.cloned.1.call-start = ((), (), s32[]{:S(2)}) async-start(), calls=%async_computation.3 | async-start | bytes 786432
Sparse Core Ops, SparseCore 0:
  425.5 179.8 reduce-scatter.4
  657.8 10.3 reduce-scatter.6
where the time goes:
time: 708 us; the launch traced here: 707 us
  local copies, waits for them, and re-layouts  363 us (51%)
  waiting for transfers between devices  192 us (27%)
  other arithmetic  76.4 us (11%)
  matrix products  54.3 us (8%)
  between operations  13.4 us (2%)
    reduce_scatter x1, waiting for transfers between devices, on_device(): lax.psum_scatter(lax.fori_loop(0, blocks_here * sub_count, one_turn, jnp....  180 us
    while x80, local copies, waits for them, and re-layouts  159 us
    another operation x16, local copies, waits for them, and re-layouts, toeplitz_rows(): repeated = jnp.tile(segment, (1, height + 1))[:, :height * (length + 1)]  83.4 us
    unnamed x4, local copies, waits for them, and re-layouts  81.4 us
    dot_general x8, matrix products, lag_product(): lax.dot_general(stacked, mixed, (((0,), (1,)), ((), ())), preferred_eleme...  54.3 us
    convert_element_type x8, other arithmetic, mix_rows(): mixed_real = (real_in * cosine + imag_in * sine_part).astype(jnp.bfloat16)  38 us
    neg x8, other arithmetic, mix_rows(): lower_half = jnp.concatenate([mixed_imag, -mixed_real], 1)  37.3 us
    slice x16, local copies, waits for them, and re-layouts, toeplitz_rows(): repeated = jnp.tile(segment, (1, height + 1))[:, :height * (length + 1)]  19.9 us
  transfers between devices with their start and end apart: 3, of which 3 were waited for; matrix products, arithmetic and copies ran while one was open for 0% of the time, Pallas kernels for 0%

commit v1 on v0

v1 whole, which is shorter than its diff:
```python
import math

import jax
import jax.numpy as jnp
import numpy as np
from jax import lax
from jax.experimental import pallas as pl
from jax.experimental.pallas import tpu as pltpu
from jax.sharding import PartitionSpec as P

F = 512
LAGS = 2048
BLOCK = 8192
STRIDED = 2048
GROUP = 4


def tables(window):
    depth = STRIDED
    phases = window // depth
    half = F // 2
    q = np.arange(half, dtype=np.float64) + 0.5
    b = np.arange(depth, dtype=np.float64)
    a = np.arange(phases, dtype=np.float64)
    inner = 2.0 * np.pi / depth * np.mod(b[:, None] * q[None, :], depth)
    waves = np.concatenate([np.cos(inner), np.sin(inner)], 1).astype(jnp.bfloat16)
    outer = 2.0 * np.pi / window * a[:, None] * q[None, :]
    scale = 1.0 / math.sqrt(window)
    turns = (np.stack([np.cos(outer), np.sin(outer)]) * scale).astype(np.float32)
    half_b = np.pi / depth * b[None, :]
    half_a = np.pi / window * a[:, None]
    return waves, turns, half_a, half_b


def kernel(lags, s_ref, r_ref, waves_ref, turns_ref, out_ref, shifted, y0, y1, u0, u1):
    phases, depth = s_ref.shape[1:]
    half = turns_ref.shape[2]
    rows = shifted.shape[2]
    per_eight = 8 // GROUP
    groups = lags // GROUP

    for early in range(8):
        for part in range(2):
            for row in range(0, rows, 8):
                shifted[early, part, row : row + 8, :] = r_ref[
                    part, row + 8 - early : row + 16 - early, :
                ]

    def build(group, y):
        eight = group // per_eight
        first = (group % per_eight) * GROUP
        start = lags - 8 - 8 * eight
        for row in range(0, phases, 16):
            here = pl.ds(pl.multiple_of(start + row, 8), 16)
            for lane in range(0, depth, 256):
                lanes = slice(lane, lane + 256)
                sr = s_ref[0, row : row + 16, lanes]
                si = s_ref[1, row : row + 16, lanes]
                for i in range(GROUP):
                    rr = shifted[first + i, 0, here, lanes]
                    ri = shifted[first + i, 1, here, lanes]
                    at = 2 * i * phases + row
                    y[at : at + 16, lanes] = (sr * rr + si * ri).astype(jnp.bfloat16)
                    at += phases
                    y[at : at + 16, lanes] = (si * rr - sr * ri).astype(jnp.bfloat16)

    def transform(y, u):
        u[...] = jnp.dot(y[...], waves_ref[...], preferred_element_type=jnp.float32)

    def gather_phases(group, u):
        for i in range(GROUP):
            for lane in range(0, half, 128):
                cos_lanes = slice(lane, lane + 128)
                sin_lanes = slice(half + lane, half + lane + 128)
                sums = [jnp.zeros((8, 128), jnp.float32) for _ in range(4)]
                for row in range(0, phases, 8):
                    c = turns_ref[0, row : row + 8, cos_lanes]
                    s = turns_ref[1, row : row + 8, cos_lanes]
                    at = 2 * i * phases + row
                    p1 = u[at : at + 8, cos_lanes]
                    p4 = u[at : at + 8, sin_lanes]
                    p3 = u[at + phases : at + phases + 8, cos_lanes]
                    p2 = u[at + phases : at + phases + 8, sin_lanes]
                    sums[0] += p1 * c - p4 * s
                    sums[1] += p2 * c + p3 * s
                    sums[2] += p3 * c - p2 * s
                    sums[3] += p4 * c + p1 * s
                al, be, ga, de = [jnp.sum(v, axis=0, keepdims=True) for v in sums]
                out_ref[group * GROUP + i, :, cos_lanes] = jnp.concatenate(
                    [al + be, ga - de, al - be, ga + de], 0
                )

    build(0, y0)

    @pl.loop(0, groups // 2)
    def _(pair):
        even = pair * 2
        transform(y0, u0)
        build(even + 1, y1)
        gather_phases(jnp.maximum(even - 1, 0), u1)
        transform(y1, u1)
        build(jnp.minimum(even + 2, groups - 1), y0)
        gather_phases(even, u0)

    gather_phases(groups - 1, u1)


def ambiguity_lags(signal, reference, first_lag, lags, interpret=False):
    window = signal.shape[1]
    depth = STRIDED
    phases = window // depth
    half = F // 2
    waves, turns, half_a, half_b = tables(window)

    strided = signal.reshape(2, depth, phases).transpose(0, 2, 1).astype(jnp.float32)
    ca, sa = [jnp.asarray(f(half_a), jnp.float32) for f in (np.cos, np.sin)]
    cb, sb = [jnp.asarray(f(half_b), jnp.float32) for f in (np.cos, np.sin)]
    c = ca * cb - sa * sb
    s = sa * cb + ca * sb
    turned = jnp.stack(
        [strided[0] * c - strided[1] * s, strided[1] * c + strided[0] * s]
    )

    padded = jnp.pad(reference, ((0, 0), (LAGS, phases)))
    delayed = lax.dynamic_slice_in_dim(
        padded, LAGS - lags - first_lag, window + phases, 1
    )
    near = delayed[:, :window].reshape(2, depth, phases)
    far = delayed[:, phases:].reshape(2, depth, phases)[:, :, :lags]
    columns = jnp.concatenate([near, far], 2).transpose(0, 2, 1).astype(jnp.float32)

    tall = GROUP * 2 * phases
    return pl.pallas_call(
        lambda *refs: kernel(lags, *refs),
        out_shape=jax.ShapeDtypeStruct((lags, 4, half), jnp.float32),
        in_specs=[pl.BlockSpec(memory_space=pltpu.VMEM)] * 4,
        out_specs=pl.BlockSpec(memory_space=pltpu.VMEM),
        scratch_shapes=[
            pltpu.VMEM((8, 2, phases + lags - 8, depth), jnp.float32),
            pltpu.VMEM((tall, depth), jnp.bfloat16),
            pltpu.VMEM((tall, depth), jnp.bfloat16),
            pltpu.VMEM((tall, F), jnp.float32),
            pltpu.VMEM((tall, F), jnp.float32),
        ],
        compiler_params=pltpu.CompilerParams(vmem_limit_bytes=56 * 1024 * 1024),
        interpret=interpret,
    )(turned, columns, jnp.asarray(waves), jnp.asarray(turns))


def everywhere(value):
    shape = value.shape
    times, cuts = lax.axis_size("tm"), lax.axis_size("dop")
    every = lax.all_gather(value, ("tm", "dop"), axis=0, tiled=False)
    every = every.reshape((times, cuts) + shape).transpose(2, 0, 3, 1, 4)
    return every.reshape(2, times * cuts * shape[1] * shape[2])


def on_device(surveillance, reference_signal):
    cuts = lax.axis_size("dop")
    lags = LAGS // (lax.axis_size("tm") * cuts)
    first_lag = (lax.axis_index("tm") * cuts + lax.axis_index("dop")) * lags
    signal = everywhere(surveillance)
    reference = everywhere(reference_signal)
    found = ambiguity_lags(signal, reference, first_lag, lags)
    whole = jnp.concatenate([found[:, 2:, ::-1], found[:, :2, :]], 2)
    return lax.all_to_all(whole, "dop", split_axis=2, concat_axis=0, tiled=True)


def solution(mesh):
    return jax.shard_map(
        on_device,
        mesh=mesh,
        in_specs=(P(None, "tm", "dop"), P(None, "tm", "dop")),
        out_specs=P("tm", None, "dop"),
        check_vma=False,
    )
```

time: 708 us -> 137 us (0.19)
  local copies, waits for them, and re-layouts: 363 us -> 11.6 us
  waiting for transfers between devices: 192 us -> 0 us
  blocking collectives: 2.17 us -> 89.8 us
  other arithmetic: 76.4 us -> 7.66 us
  matrix products: 54.3 us -> 0 us
  Pallas kernels: 0 us -> 27.4 us
  between operations: 13.4 us -> 0.2 us
    reduce_scatter x1 -> x0, waiting for transfers between devices: 180 us -> none  [on_device(): lax.psum_scatter(lax.fori_loop(0, blocks_here * sub_count, one_turn, jnp....]
    while x80 -> x0, local copies, waits for them, and re-layouts: 159 us -> none
    all_gather x1 -> x2, blocking collectives: 2.17 us -> 85.9 us  [everywhere(): every = lax.all_gather(value, ('tm', 'dop'), axis=0, tiled=False)]
    another operation x16 -> x0, local copies, waits for them, and re-layouts: 83.4 us -> none  [toeplitz_rows(): repeated = jnp.tile(segment, (1, height + 1))[:, :height * (length + 1)]]
    unnamed x4 -> x14, local copies, waits for them, and re-layouts: 81.4 us -> 1.95 us
    dot_general x8 -> x0, matrix products: 54.3 us -> none  [lag_product(): lax.dot_general(stacked, mixed, (((0,), (1,)), ((), ())), preferred_eleme...]
    neg x8 -> x0, other arithmetic: 37.3 us -> none  [mix_rows(): lower_half = jnp.concatenate([mixed_imag, -mixed_real], 1)]
    convert_element_type x8 -> x1, other arithmetic: 38 us -> 1.58 us  [ambiguity_lags(): jnp.concatenate([near, far], 2).transpose(0, 2, 1).astype(jnp.float32)]
  transfers between devices with their start and end apart: 3 -> 0, of which waited for: 3 -> 0; matrix products, arithmetic and copies ran while one was open for 0% -> 0% of each run, Pallas kernels for 0% -> 0%
where the time goes in v1:
time: 137 us
  blocking collectives  89.8 us (66%)
  Pallas kernels  27.4 us (20%)
  local copies, waits for them, and re-layouts  11.6 us (8%)
  other arithmetic  7.66 us (6%)
    all_gather x2, blocking collectives, everywhere(): every = lax.all_gather(value, ('tm', 'dop'), axis=0, tiled=False)  85.9 us
    pallas_call x1, Pallas kernels, ambiguity_lags(): pl.pallas_call(lambda *refs: kernel(lags, *refs), out_shape=jax.ShapeDtyp...  27.4 us
    all_to_all x1, blocking collectives, on_device(): return lax.all_to_all(whole, 'dop', split_axis=2, concat_axis=0, tiled=True)  3.94 us
    all_gather x1, other arithmetic, everywhere(): every = lax.all_gather(value, ('tm', 'dop'), axis=0, tiled=False)  3.15 us

profile of v1, /device:TPU:0, one launch (start us, length us, event | category | flops | bytes accessed | tf_op | source)
XLA Modules:
  0.0 136.7 jit_solution(857437413168606212)
XLA Ops:
  0.0 0.7 copy.31
  0.7 46.2 %all-gather = bf16[64,1,4096]{2,1,0:T(2,128)(2,1)S(1)} all-gather(bf16[2,1,4096]{2,1,0:T(2,128)(2,1)S(1)} %copy.31), channel_id=2, replica_groups=mesh['dop'=2,'tm'=16] {'tm','dop'}, dimensions={0}, use_global_device_ids=true | all-gather | bytes 540672 | tf_op jit(solution)/shard_map/all_gather | solution.py:153
  47.0 0.9 copy.41
  47.8 1.2 reshape.299
  49.0 0.0 copy-start
  49.0 0.6 copy.33
  49.6 0.1 copy-done
  49.8 39.7 %all-gather.1 = bf16[64,1,4096]{2,1,0:T(2,128)(2,1)S(1)} all-gather(bf16[2,1,4096]{2,1,0:T(2,128)(2,1)S(1)} %copy.34), channel_id=3, replica_groups=mesh['dop'=2,'tm'=16] {'tm','dop'}, dimensions={0}, use_global_device_ids=true | all-gather | bytes 540672 | tf_op jit(solution)/shard_map/all_gather | solution.py:153
  89.4 3.1 %reduce = bf16[64,4096]{1,0:T(8,128)(2,1)S(1)} reduce(bf16[64,1,4096]{2,1,0:T(2,128)(2,1)S(1)} %all-gather.1, bf16[]{:T(256)} %constant.48), dimensions={1}, to_apply=%all-gather.1.reduce_sub_computation | reduce | bytes 1048578 | tf_op jit(solution)/shard_map/all_gather | solution.py:153
  92.6 0.3 reshape.295
  92.9 1.5 %pad_dynamic-slice_fusion = (bf16[2,131072]{1,0:T(2,128)(2,1)S(1)}, bf16[2,131072]{1,0:T(2,128)(2,1)S(1)}) fusion(s32[]{:T(128)S(6)} %select_n.3, bf16[2,131072]{1,0:T(2,128)(2,1)S(1)} %bitcast.24, s32[]{:T(128)S(6)} %add.29), kind=kLoop, calls=%fused_computation.7 | loop fusion | bytes 1572872 | tf_op jit(solution)/shard_map/slice | solution.py:128
  94.4 0.7 reshape.298
  95.1 0.0 copy-start.1
  95.1 0.0 copy-start.2
  95.1 0.0 copy-start.3
  95.1 0.0 copy-start.4
  95.1 0.3 copy.36
  95.4 0.7 reshape.297
  96.1 0.3 copy.35
  96.4 0.0 copy-done.1
  96.5 0.0 copy-done.2
  96.5 0.0 copy-done.3
  96.5 0.0 copy-done.4
  96.5 0.3 multiply_subtract_fusion
  96.8 1.1 pad_maximum_fusion.refs_0_
  97.9 1.6 %convert_bitcast_fusion.refs_1_ = f32[2,128,2048]{2,1,0:T(8,128)} fusion(bf16[2,2048,64]{1,2,0:T(8,128)(2,1)S(1)} %copy.36, bf16[2,2048,64]{1,2,0:T(8,128)(2,1)S(1)} %copy.35), kind=kLoop, calls=%fused_computation | loop fusion | flops 2097152 | bytes 3145728 | tf_op jit(solution)/shard_map/convert_element_type | solution.py:130
  99.5 27.4 %shard_map.82 = f32[64,4,256]{2,1,0:T(4,128)} custom-call(f32[2,64,2048]{2,1,0:T(8,128)} %pad_maximum_fusion.refs_0_, f32[2,128,2048]{2,1,0:T(8,128)} %convert_bitcast_fusion.refs_1_, bf16[2048,512]{1,0:T(8,128)(2,1)} %constant.38.clone.refs_2_, f32[2,64,256]{2,1,0:T(8,128)} %constant.39.clone.refs_3_), custom_call_target="tpu_custom_call" | custom-call | tf_op jit(solution)/shard_map/pallas_call | solution.py:133
  126.9 1.1 fusion
  128.0 0.4 rev.3
  128.5 0.1 pad_maximum_fusion.1
  128.6 0.3 copy.37
  128.9 0.6 reshape.307
  129.4 3.9 %all_to_all.18 = f32[2,1,32768]{2,1,0:T(1,128)S(1)} all-to-all(f32[2,1,32768]{2,1,0:T(1,128)S(1)} %reshape.307), channel_id=1, replica_groups=mesh['dop'=2,'tm'=16] {'dop'}, dimensions={0} | all-to-all | bytes 524288 | tf_op jit(solution)/shard_map/all_to_all | solution.py:166
  133.4 0.5 broadcast.167
  133.9 1.4 %reduce.1 = f32[2,32768]{1,0:T(2,128)S(1)} reduce(f32[2,1,32768]{2,1,0:T(1,128)S(1)} %all_to_all.18, f32[]{:T(128)} %broadcast.167), dimensions={1}, to_apply=%all_to_all.13.reduce_sub_computation | reduce | bytes 524292 | tf_op jit(solution)/shard_map/all_to_all | solution.py:166
  135.3 0.5 reshape.308
  135.8 0.9 copy.38
  (1 shorter events, 0.0 us)
Async XLA Ops:
  49.0 0.7 copy-start
  95.1 1.4 %copy-start.1 = (f32[2048]{0:T(1024)S(1)}, f32[2048]{0:T(1024)}, u32[]{:S(2)}) copy-start(f32[2048]{0:T(1024)} %constant.47) | copy-start | bytes 24580
  95.1 1.4 %copy-start.2 = (f32[2048]{0:T(1024)S(1)}, f32[2048]{0:T(1024)}, u32[]{:S(2)}) copy-start(f32[2048]{0:T(1024)} %constant.45) | copy-start | bytes 24580
  95.1 1.4 %copy-start.3 = (f32[64]{0:T(128)S(1)}, f32[64]{0:T(128)}, u32[]{:S(2)}) copy-start(f32[64]{0:T(128)} %constant.46) | copy-start | bytes 772
  95.1 1.4 %copy-start.4 = (f32[64]{0:T(128)S(1)}, f32[64]{0:T(128)}, u32[]{:S(2)}) copy-start(f32[64]{0:T(128)} %constant.44) | copy-start | bytes 772

commit v2 on v1

--- a/solution.py
+++ b/solution.py
@@ -39,11 +39,14 @@
     per_eight = 8 // GROUP
     groups = lags // GROUP
 
-    for early in range(8):
-        for part in range(2):
+    @pl.loop(0, 2 * (depth // 512))
+    def _(turn):
+        part = turn % 2
+        lanes = pl.ds(pl.multiple_of(turn // 2 * 512, 512), 512)
+        for early in range(8):
             for row in range(0, rows, 8):
-                shifted[early, part, row : row + 8, :] = r_ref[
-                    part, row + 8 - early : row + 16 - early, :
+                shifted[early, part, row : row + 8, lanes] = r_ref[
+                    part, row + 8 - early : row + 16 - early, lanes
                 ]
 
     def build(group, y):
@@ -147,20 +150,103 @@
     )(turned, columns, jnp.asarray(waves), jnp.asarray(turns))
 
 
-def everywhere(value):
-    shape = value.shape
+def flipped(index, bit):
+    weight = 1 << bit
+    return index + weight * (1 - 2 * ((index // weight) % 2))
+
+
+def spread_kernel(orders, cuts, *refs):
+    count = len(orders)
+    own, every = refs[:count], refs[count : 2 * count]
+    send_sems, recv_sems = refs[2 * count :]
+    me = lax.axis_index("tm") * cuts + lax.axis_index("dop")
+
+    def place(index):
+        return {"tm": index // cuts, "dop": index % cuts}
+
+    barrier = pltpu.get_barrier_semaphore()
+    for bit in orders[0]:
+        pl.semaphore_signal(
+            barrier,
+            inc=1,
+            device_id=place(flipped(me, bit)),
+            device_id_type=pl.DeviceIdType.MESH,
+        )
+    pl.semaphore_wait(barrier, len(orders[0]))
+
+    def copy(which, source, block, slot, target):
+        return pltpu.make_async_remote_copy(
+            src_ref=source,
+            dst_ref=every[which].at[block],
+            send_sem=send_sems.at[which, slot],
+            recv_sem=recv_sems.at[which, block],
+            device_id=place(target),
+            device_id_type=pl.DeviceIdType.MESH,
+        )
+
+    sent = []
+    held = [[me] for _ in orders]
+    landed = [1] * count
+    for step in range(len(orders[0])):
+        partners = [flipped(me, order[step]) for order in orders]
+        for at in range(1 << step):
+            for which in range(count):
+                block = held[which][at]
+                mine = every[which].at[block]
+                if at == 0:
+                    mine = own[which]
+                elif at >= landed[which]:
+                    copy(which, mine, block, 0, partners[which]).wait_recv()
+                    landed[which] = at + 1
+                one = copy(which, mine, block, (1 << step) - 1 + at, partners[which])
+                one.start()
+                sent.append(one)
+        for which, order in enumerate(orders):
+            held[which] = held[which] + [flipped(h, order[step]) for h in held[which]]
+        if step == 0:
+            for which in range(count):
+                every[which][pl.ds(me, 1)] = own[which][...][None]
+    for which in range(count):
+        for at in range(landed[which], len(held[which])):
+            block = held[which][at]
+            copy(which, own[which], block, 0, flipped(me, 0)).wait_recv()
+    for one in sent:
+        one.wait_send()
+
+
+def everywhere(values):
     times, cuts = lax.axis_size("tm"), lax.axis_size("dop")
-    every = lax.all_gather(value, ("tm", "dop"), axis=0, tiled=False)
-    every = every.reshape((times, cuts) + shape).transpose(2, 0, 3, 1, 4)
-    return every.reshape(2, times * cuts * shape[1] * shape[2])
+    devices = times * cuts
+    bits = devices.bit_length() - 1
+    shape = values[0].shape
+    order = list(range(bits))[::-1]
+    other = order[:-3] + [order[-2], order[-3], order[-1]]
+    rows = shape[0] * shape[1] * shape[2] // 128
+    block = jax.ShapeDtypeStruct((devices, rows, 128), values[0].dtype)
+    gathered = pl.pallas_call(
+        lambda *refs: spread_kernel([order, other], cuts, *refs),
+        out_shape=[block] * 2,
+        in_specs=[pl.BlockSpec(memory_space=pltpu.VMEM)] * 2,
+        out_specs=[pl.BlockSpec(memory_space=pltpu.VMEM)] * 2,
+        scratch_shapes=[
+            pltpu.SemaphoreType.DMA((2, devices)),
+            pltpu.SemaphoreType.DMA((2, devices)),
+        ],
+        compiler_params=pltpu.CompilerParams(collective_id=0, has_side_effects=True),
+    )(*[value.reshape(rows, 128) for value in values])
+    return [
+        every.reshape((times, cuts) + shape)
+        .transpose(2, 0, 3, 1, 4)
+        .reshape(2, devices * shape[1] * shape[2])
+        for every in gathered
+    ]
 
 
 def on_device(surveillance, reference_signal):
     cuts = lax.axis_size("dop")
     lags = LAGS // (lax.axis_size("tm") * cuts)
     first_lag = (lax.axis_index("tm") * cuts + lax.axis_index("dop")) * lags
-    signal = everywhere(surveillance)
-    reference = everywhere(reference_signal)
+    signal, reference = everywhere([surveillance, reference_signal])
     found = ambiguity_lags(signal, reference, first_lag, lags)
     whole = jnp.concatenate([found[:, 2:, ::-1], found[:, :2, :]], 2)
     return lax.all_to_all(whole, "dop", split_axis=2, concat_axis=0, tiled=True)

time: 137 us -> 72.4 us (0.53)
  blocking collectives: 89.8 us -> 3.94 us
  Pallas kernels: 27.4 us -> 47.3 us
  local copies, waits for them, and re-layouts: 11.6 us -> 15.9 us
  other arithmetic: 7.66 us -> 4.51 us
    all_gather x2 -> x0, blocking collectives: 85.9 us -> none  [everywhere(): every = lax.all_gather(value, ('tm', 'dop'), axis=0, tiled=False)]
    pallas_call x0 -> x1, Pallas kernels: none -> 19.9 us  [everywhere(): pl.pallas_call(lambda *refs: spread_kernel([order, other], cuts, *refs),...]
    reshape x1 -> x3, local copies, waits for them, and re-layouts: 0.34 us -> 3.84 us  [the longest x2 2.68 us: everywhere(): value.reshape(rows, 128)]
    all_gather x1 -> x0, other arithmetic: 3.15 us -> none  [everywhere(): every = lax.all_gather(value, ('tm', 'dop'), axis=0, tiled=False)]
    convert_element_type x3 -> x4, local copies, waits for them, and re-layouts: 2.64 us -> 4.3 us  [ambiguity_lags(): signal.reshape(2, depth, phases).transpose(0, 2, 1).astype(jnp.float32)]
where the time goes in v2:
time: 72.4 us; the launch traced here: 71.9 us
  Pallas kernels  47.3 us (65%)
  local copies, waits for them, and re-layouts  15.9 us (22%)
  other arithmetic  4.51 us (6%)
  blocking collectives  3.94 us (5%)
    pallas_call x1, Pallas kernels, ambiguity_lags(): pl.pallas_call(lambda *refs: kernel(lags, *refs), out_shape=jax.ShapeDtyp...  27.4 us
    pallas_call x1, Pallas kernels, everywhere(): pl.pallas_call(lambda *refs: spread_kernel([order, other], cuts, *refs),...  19.9 us
    convert_element_type x4, local copies, waits for them, and re-layouts, ambiguity_lags(): signal.reshape(2, depth, phases).transpose(0, 2, 1).astype(jnp.float32)  4.3 us
    all_to_all x1, blocking collectives, on_device(): return lax.all_to_all(whole, 'dop', split_axis=2, concat_axis=0, tiled=True)  3.94 us
    reshape x2, local copies, waits for them, and re-layouts, everywhere(): value.reshape(rows, 128)  2.68 us
    convert_element_type x1, other arithmetic, ambiguity_lags(): jnp.concatenate([near, far], 2).transpose(0, 2, 1).astype(jnp.float32)  1.58 us
    slice x1, local copies, waits for them, and re-layouts, ambiguity_lags(): near = delayed[:, :window].reshape(2, depth, phases)  1.46 us

profile of v2, /device:TPU:0, one launch (start us, length us, event | category | flops | bytes accessed | tf_op | source)
XLA Modules:
  0.0 71.9 jit_solution(5462180408531810832)
XLA Ops:
  0.0 1.3 %reshape.301.refs_0_ = bf16[64,128]{1,0:T(8,128)(2,1)} reshape(bf16[2,1,4096]{2,0,1:T(2,128)(2,1)} %param.8) | data formatting | bytes 32768 | tf_op jit(solution)/shard_map/reshape | solution.py:236
  1.3 1.3 %reshape.302.refs_1_ = bf16[64,128]{1,0:T(8,128)(2,1)} reshape(bf16[2,1,4096]{2,0,1:T(2,128)(2,1)} %param.9) | data formatting | bytes 32768 | tf_op jit(solution)/shard_map/reshape | solution.py:236
  2.7 19.9 %shard_map.82 = (bf16[32,64,128]{2,1,0:T(8,128)(2,1)}, bf16[32,64,128]{2,1,0:T(8,128)(2,1)}) custom-call(bf16[64,128]{1,0:T(8,128)(2,1)} %reshape.301.refs_0_, bf16[64,128]{1,0:T(8,128)(2,1)} %reshape.302.refs_1_), custom_call_target="tpu_custom_call" | custom-call | tf_op jit(solution)/shard_map/pallas_call | solution.py:226
  22.6 1.6 %reshape.308 = f32[16,2,2,1,4096]{4,2,1,0,3:T(2,128)S(1)} reshape(bf16[32,64,128]{2,1,0:T(8,128)(2,1)} %get-tuple-element.7) | data formatting | bytes 1572864 | tf_op jit(solution)/shard_map/convert_element_type | solution.py:118
  24.2 0.9 %copy.28 = f32[16,2,2,1,4096]{4,1,0,2,3:T(2,128)S(1)} copy(f32[16,2,2,1,4096]{4,2,1,0,3:T(2,128)S(1)} %reshape.308) | data formatting | bytes 2097152 | tf_op jit(solution)/shard_map/convert_element_type | solution.py:118
  25.2 1.2 %reshape.307 = f32[2,2048,64]{2,1,0:T(8,128)S(1)} reshape(f32[2,16,1,2,4096]{4,3,1,0,2:T(2,128)S(1)} %bitcast.21) | data formatting | bytes 2097152 | tf_op jit(solution)/shard_map/convert_element_type | solution.py:118
  26.4 0.6 copy.22
  27.0 1.2 %reshape.303 = bf16[16,2,2,1,4096]{4,2,1,0,3:T(2,128)(2,1)S(1)} reshape(bf16[32,64,128]{2,1,0:T(8,128)(2,1)} %get-tuple-element.8) | data formatting | bytes 1048576 | tf_op jit(solution)/shard_map/reshape | solution.py:238
  28.1 1.5 %pad_dynamic-slice_fusion = (bf16[2,131072]{1,0:T(2,128)(2,1)S(1)}, bf16[2,131072]{1,0:T(2,128)(2,1)S(1)}) fusion(s32[]{:T(128)S(6)} %select_n.3, bf16[2,131072]{1,0:T(2,128)(2,1)S(1)} %bitcast.25, s32[]{:T(128)S(6)} %add.28), kind=kLoop, calls=%fused_computation.7 | loop fusion | bytes 1572872 | tf_op jit(solution)/shard_map/slice | solution.py:131
  29.6 0.7 reshape.306
  30.3 0.0 copy-start
  30.3 0.0 copy-start.1
  30.3 0.0 copy-start.2
  30.3 0.0 copy-start.3
  30.3 0.3 copy.24
  30.6 0.7 reshape.305
  31.3 0.3 copy.23
  31.6 0.0 copy-done
  31.7 0.0 copy-done.1
  31.7 0.0 copy-done.2
  31.7 0.0 copy-done.3
  31.7 0.3 multiply_subtract_fusion
  32.0 1.1 %pad_maximum_fusion.refs_0_ = f32[2,64,2048]{2,1,0:T(8,128)} fusion(f32[1,64,2048]{2,1,0:T(8,128)S(1)} %get-tuple-element.10, f32[1,64,2048]{2,1,0:T(8,128)S(1)} %get-tuple-element.9), kind=kLoop, calls=%fused_computation.1 | loop fusion | flops 262144 | bytes 2097152 | tf_op jit(solution)/shard_map/stack | solution.py:123
  33.1 1.6 %convert_bitcast_fusion.refs_1_ = f32[2,128,2048]{2,1,0:T(8,128)} fusion(bf16[2,2048,64]{1,2,0:T(8,128)(2,1)S(1)} %copy.24, bf16[2,2048,64]{1,2,0:T(8,128)(2,1)S(1)} %copy.23), kind=kLoop, calls=%fused_computation | loop fusion | flops 2097152 | bytes 3145728 | tf_op jit(solution)/shard_map/convert_element_type | solution.py:133
  34.6 27.4 %shard_map.83 = f32[64,4,256]{2,1,0:T(4,128)} custom-call(f32[2,64,2048]{2,1,0:T(8,128)} %pad_maximum_fusion.refs_0_, f32[2,128,2048]{2,1,0:T(8,128)} %convert_bitcast_fusion.refs_1_, bf16[2048,512]{1,0:T(8,128)(2,1)} %constant.38.clone.refs_2_, f32[2,64,256]{2,1,0:T(8,128)} %constant.39.clone.refs_3_), custom_call_target="tpu_custom_call" | custom-call | tf_op jit(solution)/shard_map/pallas_call | solution.py:136
  62.0 1.1 %fusion = (f32[64,2,256]{2,1,0:T(2,128)S(1)}, f32[64,2,256]{2,1,0:T(2,128)S(1)}) fusion(f32[64,4,256]{2,1,0:T(4,128)} %shard_map.83), kind=kLoop, calls=%fused_computation.10 | loop fusion | bytes 524288 | tf_op jit(solution)/shard_map/slice | solution.py:251
  63.2 0.4 rev.3
  63.6 0.1 pad_maximum_fusion.1
  63.8 0.3 copy.25
  64.0 0.6 reshape.309
  64.6 3.9 %all_to_all.18 = f32[2,1,32768]{2,1,0:T(1,128)S(1)} all-to-all(f32[2,1,32768]{2,1,0:T(1,128)S(1)} %reshape.309), channel_id=1, replica_groups=mesh['dop'=2,'tm'=16] {'dop'}, dimensions={0} | all-to-all | bytes 524288 | tf_op jit(solution)/shard_map/all_to_all | solution.py:252
  68.5 0.5 broadcast.166
  69.0 1.4 %reduce = f32[2,32768]{1,0:T(2,128)S(1)} reduce(f32[2,1,32768]{2,1,0:T(1,128)S(1)} %all_to_all.18, f32[]{:T(128)} %broadcast.166), dimensions={1}, to_apply=%all_to_all.13.reduce_sub_computation | reduce | bytes 524292 | tf_op jit(solution)/shard_map/all_to_all | solution.py:252
  70.5 0.5 reshape.310
  71.0 0.9 %copy.26 = f32[2,64,2,256]{3,2,1,0:T(2,128)} copy(f32[2,64,2,256]{1,2,3,0:T(2,128)S(1)} %bitcast.24) | data formatting | bytes 524288 | tf_op jit(solution)/shard_map/all_to_all | solution.py:252
Async XLA Ops:
  30.3 1.4 %copy-start = (f32[2048]{0:T(1024)S(1)}, f32[2048]{0:T(1024)}, u32[]{:S(2)}) copy-start(f32[2048]{0:T(1024)} %constant.47) | copy-start | bytes 24580
  30.3 1.4 %copy-start.1 = (f32[2048]{0:T(1024)S(1)}, f32[2048]{0:T(1024)}, u32[]{:S(2)}) copy-start(f32[2048]{0:T(1024)} %constant.45) | copy-start | bytes 24580
  30.3 1.4 %copy-start.2 = (f32[64]{0:T(128)S(1)}, f32[64]{0:T(128)}, u32[]{:S(2)}) copy-start(f32[64]{0:T(128)} %constant.46) | copy-start | bytes 772
  30.3 1.4 %copy-start.3 = (f32[64]{0:T(128)S(1)}, f32[64]{0:T(128)}, u32[]{:S(2)}) copy-start(f32[64]{0:T(128)} %constant.44) | copy-start | bytes 772

commit v3 on v2

--- a/solution.py
+++ b/solution.py
@@ -242,6 +242,61 @@
     ]
 
 
+def swap_kernel(cuts, parts, out, send_sems, recv_sems):
+    me = lax.axis_index("dop")
+    partners = [me]
+    for bit in range(cuts.bit_length() - 1):
+        partners = partners + [flipped(p, bit) for p in partners]
+    partners = partners[1:]
+
+    barrier = pltpu.get_barrier_semaphore()
+    for partner in partners:
+        pl.semaphore_signal(
+            barrier,
+            inc=1,
+            device_id={"dop": partner},
+            device_id_type=pl.DeviceIdType.MESH,
+        )
+    pl.semaphore_wait(barrier, len(partners))
+
+    def copy(source, target, owner):
+        return pltpu.make_async_remote_copy(
+            src_ref=parts.at[source],
+            dst_ref=out.at[owner],
+            send_sem=send_sems.at[target],
+            recv_sem=recv_sems.at[owner],
+            device_id={"dop": target},
+            device_id_type=pl.DeviceIdType.MESH,
+        )
+
+    for partner in partners:
+        copy(partner, partner, me).start()
+    out[pl.ds(me, 1)] = parts[pl.ds(me, 1)]
+    for partner in partners:
+        copy(partner, partner, partner).wait_recv()
+    for partner in partners:
+        copy(partner, partner, me).wait_send()
+
+
+def swapped(whole):
+    cuts = lax.axis_size("dop")
+    lags, two, bins = whole.shape
+    parts = whole.reshape(lags, two, cuts, bins // cuts).transpose(2, 0, 1, 3)
+    flat = parts.reshape(cuts, lags * two, bins // cuts)
+    out = pl.pallas_call(
+        lambda *refs: swap_kernel(cuts, *refs),
+        out_shape=jax.ShapeDtypeStruct(flat.shape, flat.dtype),
+        in_specs=[pl.BlockSpec(memory_space=pltpu.VMEM)],
+        out_specs=pl.BlockSpec(memory_space=pltpu.VMEM),
+        scratch_shapes=[
+            pltpu.SemaphoreType.DMA((cuts,)),
+            pltpu.SemaphoreType.DMA((cuts,)),
+        ],
+        compiler_params=pltpu.CompilerParams(collective_id=1, has_side_effects=True),
+    )(flat)
+    return out.reshape(cuts * lags, two, bins // cuts)
+
+
 def on_device(surveillance, reference_signal):
     cuts = lax.axis_size("dop")
     lags = LAGS // (lax.axis_size("tm") * cuts)
@@ -249,7 +304,7 @@
     signal, reference = everywhere([surveillance, reference_signal])
     found = ambiguity_lags(signal, reference, first_lag, lags)
     whole = jnp.concatenate([found[:, 2:, ::-1], found[:, :2, :]], 2)
-    return lax.all_to_all(whole, "dop", split_axis=2, concat_axis=0, tiled=True)
+    return swapped(whole)
 
 
 def solution(mesh):

time: 72.4 us -> 69.2 us (0.956)
  blocking collectives: 3.94 us -> 0 us
  Pallas kernels: 47.3 us -> 50.4 us
  other arithmetic: 4.51 us -> 3.06 us
  local copies, waits for them, and re-layouts: 15.9 us -> 15 us
    all_to_all x1 -> x0, blocking collectives: 3.94 us -> none  [on_device(): return lax.all_to_all(whole, 'dop', split_axis=2, concat_axis=0, tiled=True)]
    pallas_call x0 -> x1, Pallas kernels: none -> 3.1 us  [swapped(): pl.pallas_call(lambda *refs: swap_kernel(cuts, *refs), out_shape=jax.Shap...]
    reshape x0 -> x3, local copies, waits for them, and re-layouts: none -> 2.73 us  [the longest x1 1.8 us: swapped(): return out.reshape(cuts * lags, two, bins // cuts)]
    all_to_all x1 -> x0, other arithmetic: 1.44 us -> none  [on_device(): return lax.all_to_all(whole, 'dop', split_axis=2, concat_axis=0, tiled=True)]
    all_to_all x2 -> x0, local copies, waits for them, and re-layouts: 1.41 us -> none  [on_device(): return lax.all_to_all(whole, 'dop', split_axis=2, concat_axis=0, tiled=True)]
    reshape x1, local copies, waits for them, and re-layouts: 1.16 us -> 0.12 us  [everywhere(): every.reshape((times, cuts) + shape).transpose(2, 0, 3, 1, 4)]
    unnamed x10, local copies, waits for them, and re-layouts: 1.06 us -> 0.11 us
where the time goes in v3:
time: 69.2 us; the launch traced here: 68.6 us
  Pallas kernels  50.4 us (73%)
  local copies, waits for them, and re-layouts  15 us (22%)
  other arithmetic  3.06 us (4%)
    pallas_call x1, Pallas kernels, ambiguity_lags(): pl.pallas_call(lambda *refs: kernel(lags, *refs), out_shape=jax.ShapeDtyp...  27.4 us
    pallas_call x1, Pallas kernels, everywhere(): pl.pallas_call(lambda *refs: spread_kernel([order, other], cuts, *refs),...  19.9 us
    convert_element_type x4, local copies, waits for them, and re-layouts, ambiguity_lags(): signal.reshape(2, depth, phases).transpose(0, 2, 1).astype(jnp.float32)  4.29 us
    pallas_call x1, Pallas kernels, swapped(): pl.pallas_call(lambda *refs: swap_kernel(cuts, *refs), out_shape=jax.Shap...  3.1 us
    reshape x2, local copies, waits for them, and re-layouts, everywhere(): value.reshape(rows, 128)  2.67 us
    reshape x1, local copies, waits for them, and re-layouts, swapped(): return out.reshape(cuts * lags, two, bins // cuts)  1.8 us
    convert_element_type x1, other arithmetic, ambiguity_lags(): jnp.concatenate([near, far], 2).transpose(0, 2, 1).astype(jnp.float32)  1.58 us
    slice x1, local copies, waits for them, and re-layouts, ambiguity_lags(): near = delayed[:, :window].reshape(2, depth, phases)  1.46 us

profile of v3, /device:TPU:0, one launch (start us, length us, event | category | flops | bytes accessed | tf_op | source)
XLA Modules:
  0.0 68.6 jit_solution(13457395994113677589)
XLA Ops:
  0.0 1.3 %reshape.310.refs_0_ = bf16[64,128]{1,0:T(8,128)(2,1)} reshape(bf16[2,1,4096]{2,0,1:T(2,128)(2,1)} %param.8) | data formatting | bytes 32768 | tf_op jit(solution)/shard_map/reshape | solution.py:236
  1.3 1.3 %reshape.311.refs_1_ = bf16[64,128]{1,0:T(8,128)(2,1)} reshape(bf16[2,1,4096]{2,0,1:T(2,128)(2,1)} %param.9) | data formatting | bytes 32768 | tf_op jit(solution)/shard_map/reshape | solution.py:236
  2.7 19.9 %shard_map.82 = (bf16[32,64,128]{2,1,0:T(8,128)(2,1)}, bf16[32,64,128]{2,1,0:T(8,128)(2,1)}) custom-call(bf16[64,128]{1,0:T(8,128)(2,1)} %reshape.310.refs_0_, bf16[64,128]{1,0:T(8,128)(2,1)} %reshape.311.refs_1_), custom_call_target="tpu_custom_call" | custom-call | tf_op jit(solution)/shard_map/pallas_call | solution.py:226
  22.6 1.6 %reshape.320 = f32[16,2,2,1,4096]{4,2,1,0,3:T(2,128)S(1)} reshape(bf16[32,64,128]{2,1,0:T(8,128)(2,1)} %get-tuple-element.7) | data formatting | bytes 1572864 | tf_op jit(solution)/shard_map/convert_element_type | solution.py:118
  24.2 0.9 %copy.18 = f32[16,2,2,1,4096]{4,1,0,2,3:T(2,128)S(1)} copy(f32[16,2,2,1,4096]{4,2,1,0,3:T(2,128)S(1)} %reshape.320) | data formatting | bytes 2097152 | tf_op jit(solution)/shard_map/convert_element_type | solution.py:118
  25.2 1.2 %reshape.319 = f32[2,2048,64]{2,1,0:T(8,128)S(1)} reshape(f32[2,16,1,2,4096]{4,3,1,0,2:T(2,128)S(1)} %bitcast.22) | data formatting | bytes 2097152 | tf_op jit(solution)/shard_map/convert_element_type | solution.py:118
  26.3 0.0 copy-start.1
  26.3 0.0 copy-start.2
  26.4 0.0 copy-start.3
  26.4 0.0 copy-start.4
  26.4 0.6 copy.11
  27.0 0.1 copy-done.1
  27.1 0.0 copy-done.2
  27.1 0.0 copy-done.3
  27.1 0.0 copy-done.4
  27.1 0.0 copy-start
  27.1 0.3 multiply_subtract_fusion
  27.4 1.1 %pad_maximum_fusion.refs_0_ = f32[2,64,2048]{2,1,0:T(8,128)} fusion(f32[1,64,2048]{2,1,0:T(8,128)S(1)} %get-tuple-element.10, f32[1,64,2048]{2,1,0:T(8,128)S(1)} %get-tuple-element.9), kind=kLoop, calls=%fused_computation.1 | loop fusion | flops 262144 | bytes 2097152 | tf_op jit(solution)/shard_map/stack | solution.py:123
  28.4 0.0 copy-done
  28.5 0.1 reshape.312
  28.6 1.5 %pad_dynamic-slice_fusion = (bf16[2,131072]{1,0:T(2,128)(2,1)S(1)}, bf16[2,131072]{1,0:T(2,128)(2,1)S(1)}) fusion(s32[]{:T(128)S(6)} %select_n.3, bf16[2,131072]{1,0:T(2,128)(2,1)S(1)} %bitcast.24, s32[]{:T(128)S(6)} %add.28), kind=kLoop, calls=%fused_computation.7 | loop fusion | bytes 1572872 | tf_op jit(solution)/shard_map/slice | solution.py:131
  30.0 0.7 reshape.315
  30.7 0.3 copy.13
  31.0 0.7 reshape.314
  31.7 0.3 copy.12
  32.0 1.6 %convert_bitcast_fusion.refs_1_ = f32[2,128,2048]{2,1,0:T(8,128)} fusion(bf16[2,2048,64]{1,2,0:T(8,128)(2,1)S(1)} %copy.13, bf16[2,2048,64]{1,2,0:T(8,128)(2,1)S(1)} %copy.12), kind=kLoop, calls=%fused_computation | loop fusion | flops 2097152 | bytes 3145728 | tf_op jit(solution)/shard_map/convert_element_type | solution.py:133
  33.6 27.4 %shard_map.83 = f32[64,4,256]{2,1,0:T(4,128)} custom-call(f32[2,64,2048]{2,1,0:T(8,128)} %pad_maximum_fusion.refs_0_, f32[2,128,2048]{2,1,0:T(8,128)} %convert_bitcast_fusion.refs_1_, bf16[2048,512]{1,0:T(8,128)(2,1)} %constant.38.clone.refs_2_, f32[2,64,256]{2,1,0:T(8,128)} %constant.39.clone.refs_3_), custom_call_target="tpu_custom_call" | custom-call | tf_op jit(solution)/shard_map/pallas_call | solution.py:136
  61.0 1.1 %fusion = (f32[64,2,256]{2,1,0:T(2,128)S(1)}, f32[64,2,256]{2,1,0:T(2,128)S(1)}) fusion(f32[64,4,256]{2,1,0:T(4,128)} %shard_map.83), kind=kLoop, calls=%fused_computation.11 | loop fusion | bytes 524288 | tf_op jit(solution)/shard_map/slice | solution.py:306
  62.2 0.4 rev.3
  62.6 0.1 pad_maximum_fusion.1
  62.8 0.9 %reshape.317.refs_0_ = f32[2,128,256]{2,1,0:T(8,128)} reshape(f32[2,64,2,256]{3,2,1,0:T(2,128)S(1)} %bitcast.26) | data formatting | bytes 524288 | tf_op jit(solution)/shard_map/reshape | solution.py:285
  63.7 3.1 %shard_map.84 = f32[2,128,256]{2,1,0:T(8,128)} custom-call(f32[2,128,256]{2,1,0:T(8,128)} %reshape.317.refs_0_), custom_call_target="tpu_custom_call" | custom-call | tf_op jit(solution)/shard_map/pallas_call | solution.py:286
  66.8 1.8 %reshape.318 = f32[128,2,256]{2,1,0:T(2,128)} reshape(f32[2,128,256]{2,1,0:T(8,128)} %shard_map.84) | data formatting | bytes 524288 | tf_op jit(solution)/shard_map/reshape | solution.py:297
  (1 shorter events, 0.0 us)
Async XLA Ops:
  26.3 0.7 %copy-start.1 = (f32[2048]{0:T(1024)S(1)}, f32[2048]{0:T(1024)}, u32[]{:S(2)}) copy-start(f32[2048]{0:T(1024)} %constant.47) | copy-start | bytes 24580
  26.3 0.7 %copy-start.2 = (f32[2048]{0:T(1024)S(1)}, f32[2048]{0:T(1024)}, u32[]{:S(2)}) copy-start(f32[2048]{0:T(1024)} %constant.45) | copy-start | bytes 24580
  26.4 0.7 %copy-start.3 = (f32[64]{0:T(128)S(1)}, f32[64]{0:T(128)}, u32[]{:S(2)}) copy-start(f32[64]{0:T(128)} %constant.46) | copy-start | bytes 772
  26.4 0.7 %copy-start.4 = (f32[64]{0:T(128)S(1)}, f32[64]{0:T(128)}, u32[]{:S(2)}) copy-start(f32[64]{0:T(128)} %constant.44) | copy-start | bytes 772
  27.1 1.4 %copy-start = (bf16[32,64,128]{2,1,0:T(8,128)(2,1)S(1)}, bf16[32,64,128]{2,1,0:T(8,128)(2,1)}, u32[]{:S(2)}) copy-start(bf16[32,64,128]{2,1,0:T(8,128)(2,1)} %get-tuple-element.8) | copy-start | bytes 1572868
